TPU v7x, 256 devices: a whole 4x4x8 slice. The times are simulated.
256 devices in a mesh: af: 4 (over y), sa: 64 (over z, x, core).
Axes of the slice: x: 4, y: 4, z: 8, core: 2. Of those that a mesh axis runs over, the one named last changes fastest.
Arguments:
- data_real: bfloat16 [64, 512, 512], P('af', 'sa'), may hold values from -0.5 to 0.5
- data_imaginary: bfloat16 [64, 512, 512], P('af', 'sa'), may hold values from -0.5 to 0.5
- wavelet_real: float32 [64], P('af'), may hold values from -2.5 to 2.5
- wavelet_imaginary: float32 [64], P('af'), may hold values from -2.5 to 2.5
- primaries_real: float32 [64, 512, 512], P('af', 'sa'), may hold values from -3 to 3
- primaries_imaginary: float32 [64, 512, 512], P('af', 'sa'), may hold values from -3 to 3
Outputs:
- updated_real: float32 [64, 512, 512], P('af', 'sa')
- updated_imaginary: float32 [64, 512, 512], P('af', 'sa')
- misfit: float32 [2], replicated
All inputs are finite; a program needn't handle non-finite values.
Results may differ from a plain program's by a relative error of at most 0.0018.
Values may be sent and summed in bfloat16 or wider, within the bound.
A program may use at most 64 MiB of HBM per device.

v0:
```python
import math
import jax
import jax.numpy as jnp
from jax import lax
from jax.sharding import Mesh
from jax.sharding import PartitionSpec as P

N = 512
F = 64
ITERS = 2
SA = ("sa_0", "sa_1", "sa_2")
AF_SA = ("af", "sa_0", "sa_1", "sa_2")
STEP_LENGTH = 0.02
THRESHOLD = 0.25


def side_by_side(arrays, axis, dim, along):
    both = jnp.concatenate(arrays, axis=along)
    result, at, finished = (lax.all_gather(both, axis, axis=dim, tiled=True), 0, [])
    for a in arrays:
        finished.append(lax.slice_in_dim(result, at, at + a.shape[along], axis=along))
        at += a.shape[along]
    return tuple(finished)


def in_one_piece(arrays, axis, split_dim, concat_dim, along):
    widths = [a.shape[along] for a in arrays]
    both = jnp.concatenate(arrays, axis=along)
    result = lax.all_to_all(both, axis, split_axis=split_dim, concat_axis=concat_dim, tiled=True)
    return tuple(jnp.split(result, [sum(widths[:k]) for k in range(1, len(widths))], axis=along))


def by_axis(value, axes):
    for axis in axes:
        value = lax.psum(value, axis)
    return value


def fourier_tables(row_index, col_index):
    phase = row_index[:, None] * col_index[None, :] % F
    angle = phase.astype(jnp.float32) * (2.0 * math.pi / F)
    factor = 1.0 / math.sqrt(F)
    return (jnp.cos(angle) * factor, jnp.sin(angle) * factor)


def highest(left, right):
    return jnp.dot(left, right, precision=lax.Precision.HIGHEST, preferred_element_type=jnp.float32)


def stacked(part_real, part_imaginary):
    return jnp.concatenate(
        [part_real.astype(jnp.bfloat16), part_imaginary.astype(jnp.bfloat16)], axis=1
    )


def shrink(values):
    return values - jnp.clip(values, -THRESHOLD, THRESHOLD)


def on_device(
    data_real, data_imaginary, wavelet_real, wavelet_imaginary, primaries_real, primaries_imaginary
):
    row_count = data_real.shape[1]
    wave_real = wavelet_real[:, None, None]
    wave_imaginary = wavelet_imaginary[:, None, None]
    current_real = primaries_real
    current_imaginary = primaries_imaginary
    own_real = data_real.astype(jnp.float32)
    own_imaginary = data_imaginary.astype(jnp.float32)
    whole_real, whole_imaginary = side_by_side((data_real, data_imaginary), SA, 1, 0)
    local_sums = []
    for iteration in range(ITERS):
        left_rows = stacked(current_real, current_imaginary)
        product_real = jnp.einsum(
            "frk,fkc->frc", left_rows, whole_real, preferred_element_type=jnp.float32
        )
        product_imaginary = jnp.einsum(
            "frk,fkc->frc", left_rows, whole_imaginary, preferred_element_type=jnp.float32
        )
        forward_real = product_real[:, :row_count] - product_imaginary[:, row_count:]
        forward_imaginary = product_imaginary[:, :row_count] + product_real[:, row_count:]
        error_real = (
            own_real
            + forward_real
            - (wave_real * current_real - wave_imaginary * current_imaginary)
        )
        error_imaginary = (
            own_imaginary
            + forward_imaginary
            - (wave_real * current_imaginary + wave_imaginary * current_real)
        )
        local_sum = jnp.sum(error_real * error_real) + jnp.sum(error_imaginary * error_imaginary)
        local_sums.append(local_sum)
        error_rows = stacked(error_real, error_imaginary)
        with_real = jnp.einsum(
            "frk,fjk->frj", error_rows, whole_real, preferred_element_type=jnp.float32
        )
        with_imaginary = jnp.einsum(
            "frk,fjk->frj", error_rows, whole_imaginary, preferred_element_type=jnp.float32
        )
        back_real = with_real[:, :row_count] + with_imaginary[:, row_count:]
        back_imaginary = with_real[:, row_count:] - with_imaginary[:, :row_count]
        gradient_real = wave_real * error_real + wave_imaginary * error_imaginary - back_real
        gradient_imaginary = (
            wave_real * error_imaginary - wave_imaginary * error_real - back_imaginary
        )
        stepped_real = current_real + STEP_LENGTH * gradient_real
        stepped_imaginary = current_imaginary + STEP_LENGTH * gradient_imaginary
        trace_real, trace_imaginary = (
            lax.all_to_all(stepped_real, "af", split_axis=2, concat_axis=0, tiled=True),
            lax.all_to_all(stepped_imaginary, "af", split_axis=2, concat_axis=0, tiled=True),
        )
        block_shape = trace_real.shape
        flat_real = trace_real.reshape(F, -1)
        flat_imaginary = trace_imaginary.reshape(F, -1)
        every_index = jnp.arange(F, dtype=jnp.int32)
        cosine, sine = fourier_tables(every_index, every_index)
        time_real = highest(cosine, flat_real) - highest(sine, flat_imaginary)
        time_imaginary = highest(sine, flat_real) + highest(cosine, flat_imaginary)
        shrunk_real = shrink(time_real)
        shrunk_imaginary = shrink(time_imaginary)
        freq_real = (highest(cosine, shrunk_real) + highest(sine, shrunk_imaginary)).reshape(
            block_shape
        )
        freq_imaginary = (highest(cosine, shrunk_imaginary) - highest(sine, shrunk_real)).reshape(
            block_shape
        )
        current_real, current_imaginary = in_one_piece((freq_real, freq_imaginary), "af", 0, 2, 1)
    totals = by_axis(jnp.stack(local_sums), AF_SA)
    misfit = totals / (F * N * N)
    return (current_real, current_imaginary, misfit)


def solution(mesh):
    split = Mesh(mesh.devices.reshape(mesh.shape["af"], 8, 4, 2), ("af", "sa_0", "sa_1", "sa_2"))
    in_specs = (
        P("af", SA, None),
        P("af", SA, None),
        P("af"),
        P("af"),
        P("af", SA, None),
        P("af", SA, None),
    )
    out_specs = (P("af", SA, None), P("af", SA, None), P())
    return jax.shard_map(
        on_device, mesh=split, in_specs=in_specs, out_specs=out_specs, check_vma=False
    )
```

profile of v0, /device:TPU:1, one launch (start us, length us, event | category | flops | bytes accessed | tf_op | source)
XLA Modules:
  0.0 275.2 jit_solution(14884716040026939522)
XLA Ops:
  7.2 1.7 pad_maximum_fusion.3
  11.0 110.2 %all-gather.2.cloned.1.call-done = bf16[32,512,512]{2,1,0:T(8,128)(2,1)} async-done(((bf16[32,8,512]{2,1,0:T(8,128)(2,1)}), bf16[32,512,512]{2,1,0:T(8,128)(2,1)}) %all-gather.2.cloned.1.call-update) | async-done | bytes 16777232 | tf_op jit(solution)/shard_map/all_gather | solution.py:19
  121.1 4.7 %fusion.6 = f32[16,16,512]{2,1,0:T(8,128)S(1)} fusion(bf16[32,512,512]{2,1,0:T(8,128)(2,1)} %all-gather.2.cloned.1.call-done, bf16[16,8,512]{2,1,0:T(8,128)(2,1)S(1)} %convert_element_type.67, bf16[16,8,512]{2,1,0:T(8,128)(2,1)S(1)} %convert_element_type.66), kind=kOutput, calls=%fused_computation.6 | convolution fusion | flops 134742016 | bytes 9175040 | tf_op jit(solution)/shard_map/frk,fkc->frc/dot_general | solution.py:77
  125.9 5.3 %fusion.14 = f32[16,16,512]{2,1,0:T(8,128)S(1)} fusion(bf16[32,512,512]{2,1,0:T(8,128)(2,1)} %all-gather.2.cloned.1.call-done, bf16[16,8,512]{2,1,0:T(8,128)(2,1)S(1)} %convert_element_type.67, bf16[16,8,512]{2,1,0:T(8,128)(2,1)S(1)} %convert_element_type.66), kind=kOutput, calls=%fused_computation.14 | convolution fusion | flops 134742016 | bytes 9175040 | tf_op jit(solution)/shard_map/frk,fkc->frc/dot_general | solution.py:74
  132.1 2.3 fusion.4
  134.4 2.3 fusion.12
  137.8 1.5 reshape.44
  139.2 4.0 %all-to-all-start = ((f32[4,1,16384]{2,1,0:T(1,128)}), f32[4,1,16384]{2,1,0:T(1,128)S(1)}, u32[]{:S(2)}, u32[]{:S(2)}) async-start(f32[4,1,16384]{2,1,0:T(1,128)} %reshape.44), calls=%async_computation | async-start | bytes 524288 | tf_op jit(solution)/shard_map/all_to_all | solution.py:110
  144.0 1.5 reshape.46
  145.5 3.6 %all-to-all-done = f32[4,1,16384]{2,1,0:T(1,128)S(1)} async-done(((f32[4,1,16384]{2,1,0:T(1,128)}), f32[4,1,16384]{2,1,0:T(1,128)S(1)}, u32[]{:S(2)}, u32[]{:S(2)}) %all-to-all-start) | async-done | bytes 262176 | tf_op jit(solution)/shard_map/all_to_all | solution.py:110
  149.1 3.6 %all-to-all-start.1 = ((f32[4,1,16384]{2,1,0:T(1,128)}), f32[4,1,16384]{2,1,0:T(1,128)S(1)}, u32[]{:S(2)}, u32[]{:S(2)}) async-start(f32[4,1,16384]{2,1,0:T(1,128)} %reshape.46), calls=%async_computation.1 | async-start | bytes 524288 | tf_op jit(solution)/shard_map/all_to_all | solution.py:111
  153.3 1.4 reduce
  157.0 1.0 all-to-all-done.1
  158.1 1.4 reduce.1
  164.0 9.7 %all_to_all.96 = f32[64,16,128]{2,1,0:T(8,128)S(1)} all-to-all(f32[64,16,128]{2,1,0:T(8,128)S(1)} %pad_maximum_fusion), channel_id=1, replica_groups=mesh['af'=4,'sa_0'=8,'sa_1'=4,'sa_2'=2] {'af'}, dimensions={0} | all-to-all | bytes 1048576 | tf_op jit(solution)/shard_map/all_to_all | solution.py:29
  173.9 4.7 %fusion.2 = f32[16,16,512]{2,1,0:T(8,128)S(1)} fusion(bf16[32,512,512]{2,1,0:T(8,128)(2,1)} %all-gather.2.cloned.1.call-done, bf16[16,8,512]{2,1,0:T(8,128)(2,1)S(1)} %get-tuple-element.22, bf16[16,8,512]{2,1,0:T(8,128)(2,1)S(1)} %get-tuple-element.21), kind=kOutput, calls=%fused_computation.2 | convolution fusion | flops 134742016 | bytes 9175040 | tf_op jit(solution)/shard_map/frk,fkc->frc/dot_general | solution.py:77
  178.6 4.7 %fusion.10 = f32[16,16,512]{2,1,0:T(8,128)S(1)} fusion(bf16[32,512,512]{2,1,0:T(8,128)(2,1)} %all-gather.2.cloned.1.call-done, bf16[16,8,512]{2,1,0:T(8,128)(2,1)S(1)} %get-tuple-element.22, bf16[16,8,512]{2,1,0:T(8,128)(2,1)S(1)} %get-tuple-element.21), kind=kOutput, calls=%fused_computation.10 | convolution fusion | flops 134742016 | bytes 9175040 | tf_op jit(solution)/shard_map/frk,fkc->frc/dot_general | solution.py:74
  184.3 2.3 fusion
  186.6 2.3 fusion.8
  190.0 1.5 reshape.48
  191.4 3.4 %all-to-all-start.3 = ((f32[4,1,16384]{2,1,0:T(1,128)}), f32[4,1,16384]{2,1,0:T(1,128)S(1)}, u32[]{:S(2)}, u32[]{:S(2)}) async-start(f32[4,1,16384]{2,1,0:T(1,128)} %reshape.48), calls=%async_computation.3 | async-start | bytes 524288 | tf_op jit(solution)/shard_map/all_to_all | solution.py:110
  195.7 1.5 reshape.50
  197.1 3.2 %all-to-all-done.3 = f32[4,1,16384]{2,1,0:T(1,128)S(1)} async-done(((f32[4,1,16384]{2,1,0:T(1,128)}), f32[4,1,16384]{2,1,0:T(1,128)S(1)}, u32[]{:S(2)}, u32[]{:S(2)}) %all-to-all-start.3) | async-done | bytes 262176 | tf_op jit(solution)/shard_map/all_to_all | solution.py:110
  200.3 3.7 %all-to-all-start.4 = ((f32[4,1,16384]{2,1,0:T(1,128)}), f32[4,1,16384]{2,1,0:T(1,128)S(1)}, u32[]{:S(2)}, u32[]{:S(2)}) async-start(f32[4,1,16384]{2,1,0:T(1,128)} %reshape.50), calls=%async_computation.4 | async-start | bytes 524288 | tf_op jit(solution)/shard_map/all_to_all | solution.py:111
  204.0 1.4 reduce.2
  207.7 1.5 all-to-all-done.4
  209.2 1.4 reduce.3
  216.0 3.5 %all-to-all-start.5 = ((f32[64,16,128]{2,1,0:T(8,128)}), f32[64,16,128]{2,1,0:T(8,128)S(1)}, u32[]{:S(2)}, u32[]{:S(2)}) async-start(f32[64,16,128]{2,1,0:T(8,128)} %pad_maximum_fusion.1), calls=%async_computation.5 | async-start | bytes 1048576 | tf_op jit(solution)/shard_map/all_to_all | solution.py:29
  222.0 9.3 %psum.28 = f32[2]{0:T(128)S(1)} all-reduce(f32[2]{0:T(128)S(1)} %pad_maximum_fusion.15), channel_id=1, replica_groups=mesh['af'=4,'sa_0'=8,'sa_1'=4,'sa_2'=2] {'af'}, use_global_device_ids=true, to_apply=%region_4.5 | all-reduce | flops 2 | bytes 16 | tf_op jit(solution)/shard_map/psum | solution.py:35
  231.3 12.5 %psum.29 = f32[2]{0:T(128)S(1)} all-reduce(f32[2]{0:T(128)S(1)} %psum.28), channel_id=1, replica_groups=mesh['af'=4,'sa_0'=8,'sa_1'=4,'sa_2'=2] {'sa_0'}, use_global_device_ids=true, to_apply=%region_5.6 | all-reduce | flops 2 | bytes 16 | tf_op jit(solution)/shard_map/psum | solution.py:35
  243.8 7.2 %psum.30 = f32[2]{0:T(128)S(1)} all-reduce(f32[2]{0:T(128)S(1)} %psum.29), channel_id=1, replica_groups=mesh['af'=4,'sa_0'=8,'sa_1'=4,'sa_2'=2] {'sa_1'}, use_global_device_ids=true, to_apply=%region_6.7 | all-reduce | flops 2 | bytes 16 | tf_op jit(solution)/shard_map/psum | solution.py:35
  251.1 15.4 %psum.31 = f32[2]{0:T(128)S(1)} all-reduce(f32[2]{0:T(128)S(1)} %psum.30), channel_id=1, replica_groups=mesh['af'=4,'sa_0'=8,'sa_1'=4,'sa_2'=2] {'sa_2'}, use_global_device_ids=true, to_apply=%region_7.8 | all-reduce | flops 2 | bytes 16 | tf_op jit(solution)/shard_map/psum | solution.py:35
  (78 shorter events, 24.7 us)
Async XLA Ops:
  7.2 114.0 %all-gather.2.cloned.1.call-start = ((), (), s32[]{:S(2)}) async-start(), calls=%async_computation.6 | async-start | bytes 17039360 | tf_op jit(solution)/shard_map/all_gather | solution.py:19
  10.9 120.3 %copy-start.1 = (f32[16,8,512]{2,1,0:T(8,128)S(1)}, f32[16,8,512]{2,1,0:T(8,128)}, u32[]{:S(2)}) copy-start(f32[16,8,512]{2,1,0:T(8,128)} %param.11) | copy-start | bytes 786436
  10.9 120.3 %copy-start.2 = (f32[16,8,512]{2,1,0:T(8,128)S(1)}, f32[16,8,512]{2,1,0:T(8,128)}, u32[]{:S(2)}) copy-start(f32[16,8,512]{2,1,0:T(8,128)} %param.10) | copy-start | bytes 786436
  10.9 120.3 %copy-start.3 = (bf16[16,8,512]{2,1,0:T(8,128)(2,1)S(1)}, bf16[16,8,512]{2,1,0:T(8,128)(2,1)}, u32[]{:S(2)}) copy-start(bf16[16,8,512]{2,1,0:T(8,128)(2,1)} %param.7) | copy-start | bytes 393220
  10.9 120.3 %copy-start.4 = (bf16[16,8,512]{2,1,0:T(8,128)(2,1)S(1)}, bf16[16,8,512]{2,1,0:T(8,128)(2,1)}, u32[]{:S(2)}) copy-start(bf16[16,8,512]{2,1,0:T(8,128)(2,1)} %param.6) | copy-start | bytes 393220
  10.9 120.3 %copy-start.5 = (f32[16]{0:T(128)S(1)}, f32[16]{0:T(128)}, u32[]{:S(2)}) copy-start(f32[16]{0:T(128)} %param.9) | copy-start | bytes 196
  10.9 120.3 %copy-start.6 = (f32[16]{0:T(128)S(1)}, f32[16]{0:T(128)}, u32[]{:S(2)}) copy-start(f32[16]{0:T(128)} %param.8) | copy-start | bytes 196
  121.1 11.0 %copy-start = (bf16[32,512,512]{2,1,0:T(8,128)(2,1)S(1)}, bf16[32,512,512]{2,1,0:T(8,128)(2,1)}, u32[]{:S(2)}) copy-start(bf16[32,512,512]{2,1,0:T(8,128)(2,1)} %all-gather.2.cloned.1.call-done) | copy-start | bytes 50331652
  139.2 9.9 %all-to-all-start = ((f32[4,1,16384]{2,1,0:T(1,128)}), f32[4,1,16384]{2,1,0:T(1,128)S(1)}, u32[]{:S(2)}, u32[]{:S(2)}) async-start(f32[4,1,16384]{2,1,0:T(1,128)} %reshape.44), calls=%async_computation | async-start | bytes 524288 | tf_op jit(solution)/shard_map/all_to_all | solution.py:110
  149.1 8.9 %all-to-all-start.1 = ((f32[4,1,16384]{2,1,0:T(1,128)}), f32[4,1,16384]{2,1,0:T(1,128)S(1)}, u32[]{:S(2)}, u32[]{:S(2)}) async-start(f32[4,1,16384]{2,1,0:T(1,128)} %reshape.46), calls=%async_computation.1 | async-start | bytes 524288 | tf_op jit(solution)/shard_map/all_to_all | solution.py:111
  160.7 23.6 %slice-start = ((s8[16777216]{0:T(1024)(128)(4,1)}), s8[4194304]{0:T(1024)(128)(4,1)S(1)}, s32[]{:S(2)}) async-start(s8[16777216]{0:T(1024)(128)(4,1)} %bitcast.77), calls=%async_computation.7 | async-start | bytes 8388608
  173.7 10.6 %slice-start.1 = ((s8[16777216]{0:T(1024)(128)(4,1)}), s8[4194304]{0:T(1024)(128)(4,1)S(1)}, s32[]{:S(2)}) async-start(s8[16777216]{0:T(1024)(128)(4,1)} %bitcast.77), calls=%async_computation.8 | async-start | bytes 8388608
  173.9 10.5 %slice-start.2 = ((s8[16777216]{0:T(1024)(128)(4,1)}), s8[4194304]{0:T(1024)(128)(4,1)S(1)}, s32[]{:S(2)}) async-start(s8[16777216]{0:T(1024)(128)(4,1)} %bitcast.77), calls=%async_computation.9 | async-start | bytes 8388608
  178.6 5.7 %slice-start.3 = ((s8[16777216]{0:T(1024)(128)(4,1)}), s8[4194304]{0:T(1024)(128)(4,1)S(1)}, s32[]{:S(2)}) async-start(s8[16777216]{0:T(1024)(128)(4,1)} %bitcast.77), calls=%async_computation.10 | async-start | bytes 8388608
  191.4 8.9 %all-to-all-start.3 = ((f32[4,1,16384]{2,1,0:T(1,128)}), f32[4,1,16384]{2,1,0:T(1,128)S(1)}, u32[]{:S(2)}, u32[]{:S(2)}) async-start(f32[4,1,16384]{2,1,0:T(1,128)} %reshape.48), calls=%async_computation.3 | async-start | bytes 524288 | tf_op jit(solution)/shard_map/all_to_all | solution.py:110
  200.3 8.9 %all-to-all-start.4 = ((f32[4,1,16384]{2,1,0:T(1,128)}), f32[4,1,16384]{2,1,0:T(1,128)S(1)}, u32[]{:S(2)}, u32[]{:S(2)}) async-start(f32[4,1,16384]{2,1,0:T(1,128)} %reshape.50), calls=%async_computation.4 | async-start | bytes 524288 | tf_op jit(solution)/shard_map/all_to_all | solution.py:111
  216.0 51.0 %all-to-all-start.5 = ((f32[64,16,128]{2,1,0:T(8,128)}), f32[64,16,128]{2,1,0:T(8,128)S(1)}, u32[]{:S(2)}, u32[]{:S(2)}) async-start(f32[64,16,128]{2,1,0:T(8,128)} %pad_maximum_fusion.1), calls=%async_computation.5 | async-start | bytes 1048576 | tf_op jit(solution)/shard_map/all_to_all | solution.py:29
Sparse Core Ops, SparseCore 0:
  11.2 109.8 all-gather.1
where the time goes:
time: 276 us; the launch traced here: 275 us
  waiting for transfers between devices  120 us (43%)
  blocking collectives  54.1 us (20%)
  matrix products  37 us (13%)
  starting transfers between devices  18.2 us (7%)
  between operations  17 us (6%)
  local copies, waits for them, and re-layouts  16.5 us (6%)
  other arithmetic  12.8 us (5%)
    all_gather x1, waiting for transfers between devices, side_by_side(): lax.all_gather(both, axis, axis=dim, tiled=True)  110 us
    psum x4, blocking collectives, by_axis(): value = lax.psum(value, axis)  44.4 us
    dot_general x2, matrix products, on_device(): jnp.einsum('frk,fkc->frc', left_rows, whole_real, preferred_element_type=...  10.1 us
    all_to_all x1, blocking collectives, in_one_piece(): lax.all_to_all(both, axis, split_axis=split_dim, concat_axis=concat_dim,...  9.72 us
    dot_general x2, matrix products, on_device(): jnp.einsum('frk,fkc->frc', left_rows, whole_imaginary, preferred_element_...  9.44 us
    unnamed x34, local copies, waits for them, and re-layouts  8.78 us
    dot_general x16, matrix products, highest(): jnp.dot(left, right, precision=lax.Precision.HIGHEST, preferred_element_t...  8.37 us
    all_to_all x2, starting transfers between devices, on_device(): lax.all_to_all(stepped_real, 'af', split_axis=2, concat_axis=0, tiled=True)  7.41 us
  transfers between devices with their start and end apart: 6, of which 5 were waited for; matrix products, arithmetic and copies ran while one was open for 5% of the time, Pallas kernels for 0%

commit v1 on v0

--- a/solution.py
+++ b/solution.py
@@ -4,6 +4,7 @@
 from jax import lax
 from jax.sharding import Mesh
 from jax.sharding import PartitionSpec as P
+from jax.lax import axis_index, axis_size, ppermute
 
 N = 512
 F = 64
@@ -12,6 +13,28 @@
 AF_SA = ("af", "sa_0", "sa_1", "sa_2")
 STEP_LENGTH = 0.02
 THRESHOLD = 0.25
+
+
+def save_tasks(x_in, axis_name, on_dim, d_out):
+    long_array = axis_size(axis_name)
+    answer = axis_index(axis_name)
+    arr_now, piece_out = (long_array, answer)
+    outcome_arr = x_in.shape[on_dim] // arr_now
+    fresh = list(x_in.shape)
+    fresh[on_dim] = outcome_arr
+    u1 = fresh[d_out]
+    fresh[d_out] = u1 * arr_now
+    vec_out = jnp.zeros(fresh, x_in.dtype)
+    dd = 0
+    while dd < arr_now:
+        h_now = lax.dynamic_slice_in_dim(
+            x_in, (piece_out ^ dd) * outcome_arr, outcome_arr, axis=on_dim
+        )
+        if dd:
+            h_now = ppermute(h_now, axis_name=axis_name, perm=[(b, b ^ dd) for b in range(arr_now)])
+        vec_out = lax.dynamic_update_slice_in_dim(vec_out, h_now, (piece_out ^ dd) * u1, axis=d_out)
+        dd = dd + 1
+    return vec_out
 
 
 def side_by_side(arrays, axis, dim, along):
@@ -107,7 +130,7 @@
         stepped_real = current_real + STEP_LENGTH * gradient_real
         stepped_imaginary = current_imaginary + STEP_LENGTH * gradient_imaginary
         trace_real, trace_imaginary = (
-            lax.all_to_all(stepped_real, "af", split_axis=2, concat_axis=0, tiled=True),
+            save_tasks(stepped_real, "af", 2, 0),
             lax.all_to_all(stepped_imaginary, "af", split_axis=2, concat_axis=0, tiled=True),
         )
         block_shape = trace_real.shape

time: 276 us -> 267 us (0.967)
  local copies, waits for them, and re-layouts: 16.5 us -> 9.59 us
  other arithmetic: 12.8 us -> 9.97 us
    ppermute x0 -> x6, waiting for transfers between devices: none -> 11.2 us  [save_tasks(): ppermute(h_now, axis_name=axis_name, perm=[(b, b ^ dd) for b in range(arr...]
    ppermute x0 -> x6, starting transfers between devices: none -> 9.39 us  [save_tasks(): ppermute(h_now, axis_name=axis_name, perm=[(b, b ^ dd) for b in range(arr...]
    all_to_all x2 -> x0, starting transfers between devices: 7.41 us -> none  [on_device(): lax.all_to_all(stepped_real, 'af', split_axis=2, concat_axis=0, tiled=True)]
    all_to_all x2 -> x0, waiting for transfers between devices: 6.86 us -> none  [on_device(): lax.all_to_all(stepped_real, 'af', split_axis=2, concat_axis=0, tiled=True)]
    psum x4, blocking collectives: 44.4 us -> 40.1 us  [by_axis(): value = lax.psum(value, axis)]
    unnamed x34 -> x30, local copies, waits for them, and re-layouts: 8.78 us -> 4.52 us
  transfers between devices with their start and end apart: 6 -> 10, of which waited for: 5 -> 5; matrix products, arithmetic and copies ran while one was open for 5% -> 3% of each run, Pallas kernels for 0% -> 0%
where the time goes in v1:
time: 267 us
  waiting for transfers between devices  121 us (45%)
  blocking collectives  51.6 us (19%)
  matrix products  37 us (14%)
  starting transfers between devices  20 us (7%)
  between operations  17 us (6%)
  other arithmetic  9.97 us (4%)
  local copies, waits for them, and re-layouts  9.59 us (4%)
    all_gather x1, waiting for transfers between devices, side_by_side(): lax.all_gather(both, axis, axis=dim, tiled=True)  110 us
    psum x4, blocking collectives, by_axis(): value = lax.psum(value, axis)  40.1 us
    all_to_all x1, blocking collectives, in_one_piece(): lax.all_to_all(both, axis, split_axis=split_dim, concat_axis=concat_dim,...  11.5 us
    ppermute x6, waiting for transfers between devices, save_tasks(): ppermute(h_now, axis_name=axis_name, perm=[(b, b ^ dd) for b in range(arr...  11.2 us
    dot_general x2, matrix products, on_device(): jnp.einsum('frk,fkc->frc', left_rows, whole_real, preferred_element_type=...  10.1 us
    dot_general x2, matrix products, on_device(): jnp.einsum('frk,fkc->frc', left_rows, whole_imaginary, preferred_element_...  9.44 us
    ppermute x6, starting transfers between devices, save_tasks(): ppermute(h_now, axis_name=axis_name, perm=[(b, b ^ dd) for b in range(arr...  9.39 us
    dot_general x16, matrix products, highest(): jnp.dot(left, right, precision=lax.Precision.HIGHEST, preferred_element_t...  8.38 us
  transfers between devices with their start and end apart: 10, of which 5 were waited for; matrix products, arithmetic and copies ran while one was open for 3% of the time, Pallas kernels for 0%

profile of v1, /device:TPU:1, one launch (start us, length us, event | category | flops | bytes accessed | tf_op | source)
XLA Modules:
  0.0 266.6 jit_solution(15404997561926255603)
XLA Ops:
  7.2 1.7 pad_maximum_fusion.3
  8.9 1.0 convert_element_type.67
  9.9 1.0 convert_element_type.66
  11.0 110.1 %all-gather.2.cloned.1.call-done = bf16[32,512,512]{2,1,0:T(8,128)(2,1)} async-done(((bf16[32,8,512]{2,1,0:T(8,128)(2,1)}), bf16[32,512,512]{2,1,0:T(8,128)(2,1)}) %all-gather.2.cloned.1.call-update) | async-done | bytes 16777232 | tf_op jit(solution)/shard_map/all_gather | solution.py:42
  121.1 4.7 %fusion.6 = f32[16,16,512]{2,1,0:T(8,128)S(1)} fusion(bf16[32,512,512]{2,1,0:T(8,128)(2,1)} %all-gather.2.cloned.1.call-done, bf16[16,8,512]{2,1,0:T(8,128)(2,1)S(1)} %convert_element_type.67, bf16[16,8,512]{2,1,0:T(8,128)(2,1)S(1)} %convert_element_type.66), kind=kOutput, calls=%fused_computation.6 | convolution fusion | flops 134742016 | bytes 9175040 | tf_op jit(solution)/shard_map/frk,fkc->frc/dot_general | solution.py:100
  125.9 5.3 %fusion.14 = f32[16,16,512]{2,1,0:T(8,128)S(1)} fusion(bf16[32,512,512]{2,1,0:T(8,128)(2,1)} %all-gather.2.cloned.1.call-done, bf16[16,8,512]{2,1,0:T(8,128)(2,1)S(1)} %convert_element_type.67, bf16[16,8,512]{2,1,0:T(8,128)(2,1)S(1)} %convert_element_type.66), kind=kOutput, calls=%fused_computation.14 | convolution fusion | flops 134742016 | bytes 9175040 | tf_op jit(solution)/shard_map/frk,fkc->frc/dot_general | solution.py:97
  132.1 2.3 fusion.4
  134.4 2.3 fusion.12
  137.0 1.3 collective-permute-start
  139.1 1.5 reshape.42
  140.6 3.7 %all-to-all-start = ((f32[4,1,16384]{2,1,0:T(1,128)}), f32[4,1,16384]{2,1,0:T(1,128)S(1)}, u32[]{:S(2)}, u32[]{:S(2)}) async-start(f32[4,1,16384]{2,1,0:T(1,128)} %reshape.42), calls=%async_computation | async-start | bytes 524288 | tf_op jit(solution)/shard_map/all_to_all | solution.py:134
  144.3 3.0 %collective-permute-start.1 = (f32[16,8,128]{2,1,0:T(8,128)S(1)}, f32[16,8,128]{2,1,0:T(8,128)S(1)}, u32[]{:S(2)}, u32[]{:S(2)}) collective-permute-start(f32[16,8,128]{2,1,0:T(8,128)S(1)} %get-tuple-element.28), channel_id=1, source_target_pairs={{0,128},{64,192},{128,0},{192,64},{1,129},{65,193},{129,1},{193,65... | collective-permute-start | bytes 196616 | tf_op jit(solution)/shard_map/ppermute | solution.py:34
  148.2 3.5 %collective-permute-done.1 = f32[16,8,128]{2,1,0:T(8,128)S(1)} collective-permute-done((f32[16,8,128]{2,1,0:T(8,128)S(1)}, f32[16,8,128]{2,1,0:T(8,128)S(1)}, u32[]{:S(2)}, u32[]{:S(2)}) %collective-permute-start.1) | collective-permute-done | bytes 65568 | tf_op jit(solution)/shard_map/ppermute | solution.py:34
  151.7 2.6 collective-permute-done.2
  154.8 1.3 reduce
  161.8 11.5 %all_to_all.66 = f32[64,16,128]{2,1,0:T(8,128)S(1)} all-to-all(f32[64,16,128]{2,1,0:T(8,128)S(1)} %pad_maximum_fusion), channel_id=1, replica_groups=mesh['af'=4,'sa_0'=8,'sa_1'=4,'sa_2'=2] {'af'}, dimensions={0} | all-to-all | bytes 1048576 | tf_op jit(solution)/shard_map/all_to_all | solution.py:52
  173.4 4.7 %fusion.2 = f32[16,16,512]{2,1,0:T(8,128)S(1)} fusion(bf16[32,512,512]{2,1,0:T(8,128)(2,1)} %all-gather.2.cloned.1.call-done, bf16[16,8,512]{2,1,0:T(8,128)(2,1)S(1)} %get-tuple-element.22, bf16[16,8,512]{2,1,0:T(8,128)(2,1)S(1)} %get-tuple-element.21), kind=kOutput, calls=%fused_computation.2 | convolution fusion | flops 134742016 | bytes 9175040 | tf_op jit(solution)/shard_map/frk,fkc->frc/dot_general | solution.py:100
  178.2 4.7 %fusion.10 = f32[16,16,512]{2,1,0:T(8,128)S(1)} fusion(bf16[32,512,512]{2,1,0:T(8,128)(2,1)} %all-gather.2.cloned.1.call-done, bf16[16,8,512]{2,1,0:T(8,128)(2,1)S(1)} %get-tuple-element.22, bf16[16,8,512]{2,1,0:T(8,128)(2,1)S(1)} %get-tuple-element.21), kind=kOutput, calls=%fused_computation.10 | convolution fusion | flops 134742016 | bytes 9175040 | tf_op jit(solution)/shard_map/frk,fkc->frc/dot_general | solution.py:97
  183.8 2.3 fusion
  186.1 2.3 fusion.8
  189.9 1.5 reshape.44
  191.4 3.4 %all-to-all-start.2 = ((f32[4,1,16384]{2,1,0:T(1,128)}), f32[4,1,16384]{2,1,0:T(1,128)S(1)}, u32[]{:S(2)}, u32[]{:S(2)}) async-start(f32[4,1,16384]{2,1,0:T(1,128)} %reshape.44), calls=%async_computation.2 | async-start | bytes 524288 | tf_op jit(solution)/shard_map/all_to_all | solution.py:134
  194.8 2.9 %collective-permute-start.4 = (f32[16,8,128]{2,1,0:T(8,128)S(1)}, f32[16,8,128]{2,1,0:T(8,128)S(1)}, u32[]{:S(2)}, u32[]{:S(2)}) collective-permute-start(f32[16,8,128]{2,1,0:T(8,128)S(1)} %get-tuple-element.24), channel_id=1, source_target_pairs={{0,128},{64,192},{128,0},{192,64},{1,129},{65,193},{129,1},{193,65... | collective-permute-start | bytes 196616 | tf_op jit(solution)/shard_map/ppermute | solution.py:34
  197.7 0.9 collective-permute-start.5
  198.7 2.3 collective-permute-done.4
  201.0 2.8 %collective-permute-done.5 = f32[16,8,128]{2,1,0:T(8,128)S(1)} collective-permute-done((f32[16,8,128]{2,1,0:T(8,128)S(1)}, f32[16,8,128]{2,1,0:T(8,128)S(1)}, u32[]{:S(2)}, u32[]{:S(2)}) %collective-permute-start.5) | collective-permute-done | bytes 65568 | tf_op jit(solution)/shard_map/ppermute | solution.py:34
  203.8 1.3 reduce.1
  211.7 3.5 %all-to-all-start.3 = ((f32[64,16,128]{2,1,0:T(8,128)}), f32[64,16,128]{2,1,0:T(8,128)S(1)}, u32[]{:S(2)}, u32[]{:S(2)}) async-start(f32[64,16,128]{2,1,0:T(8,128)} %pad_maximum_fusion.1), calls=%async_computation.3 | async-start | bytes 1048576 | tf_op jit(solution)/shard_map/all_to_all | solution.py:52
  217.7 9.4 %psum.28 = f32[2]{0:T(128)S(1)} all-reduce(f32[2]{0:T(128)S(1)} %pad_maximum_fusion.15), channel_id=1, replica_groups=mesh['af'=4,'sa_0'=8,'sa_1'=4,'sa_2'=2] {'af'}, use_global_device_ids=true, to_apply=%region_4.5 | all-reduce | flops 2 | bytes 16 | tf_op jit(solution)/shard_map/psum | solution.py:58
  227.1 12.5 %psum.29 = f32[2]{0:T(128)S(1)} all-reduce(f32[2]{0:T(128)S(1)} %psum.28), channel_id=1, replica_groups=mesh['af'=4,'sa_0'=8,'sa_1'=4,'sa_2'=2] {'sa_0'}, use_global_device_ids=true, to_apply=%region_5.6 | all-reduce | flops 2 | bytes 16 | tf_op jit(solution)/shard_map/psum | solution.py:58
  239.6 7.3 %psum.30 = f32[2]{0:T(128)S(1)} all-reduce(f32[2]{0:T(128)S(1)} %psum.29), channel_id=1, replica_groups=mesh['af'=4,'sa_0'=8,'sa_1'=4,'sa_2'=2] {'sa_1'}, use_global_device_ids=true, to_apply=%region_6.7 | all-reduce | flops 2 | bytes 16 | tf_op jit(solution)/shard_map/psum | solution.py:58
  246.9 10.9 %psum.31 = f32[2]{0:T(128)S(1)} all-reduce(f32[2]{0:T(128)S(1)} %psum.30), channel_id=1, replica_groups=mesh['af'=4,'sa_0'=8,'sa_1'=4,'sa_2'=2] {'sa_2'}, use_global_device_ids=true, to_apply=%region_7.8 | all-reduce | flops 2 | bytes 16 | tf_op jit(solution)/shard_map/psum | solution.py:58
  (86 shorter events, 20.0 us)
Async XLA Ops:
  7.2 114.0 %all-gather.2.cloned.1.call-start = ((), (), s32[]{:S(2)}) async-start(), calls=%async_computation.4 | async-start | bytes 17039360 | tf_op jit(solution)/shard_map/all_gather | solution.py:42
  10.9 120.3 %copy-start.1 = (f32[16,8,512]{2,1,0:T(8,128)S(1)}, f32[16,8,512]{2,1,0:T(8,128)}, u32[]{:S(2)}) copy-start(f32[16,8,512]{2,1,0:T(8,128)} %param.10) | copy-start | bytes 786436
  10.9 120.3 %copy-start.2 = (f32[16,8,512]{2,1,0:T(8,128)S(1)}, f32[16,8,512]{2,1,0:T(8,128)}, u32[]{:S(2)}) copy-start(f32[16,8,512]{2,1,0:T(8,128)} %param.11) | copy-start | bytes 786436
  10.9 120.3 %copy-start.3 = (bf16[16,8,512]{2,1,0:T(8,128)(2,1)S(1)}, bf16[16,8,512]{2,1,0:T(8,128)(2,1)}, u32[]{:S(2)}) copy-start(bf16[16,8,512]{2,1,0:T(8,128)(2,1)} %param.7) | copy-start | bytes 393220
  10.9 120.3 %copy-start.4 = (bf16[16,8,512]{2,1,0:T(8,128)(2,1)S(1)}, bf16[16,8,512]{2,1,0:T(8,128)(2,1)}, u32[]{:S(2)}) copy-start(bf16[16,8,512]{2,1,0:T(8,128)(2,1)} %param.6) | copy-start | bytes 393220
  11.0 120.3 %copy-start.5 = (f32[16]{0:T(128)S(1)}, f32[16]{0:T(128)}, u32[]{:S(2)}) copy-start(f32[16]{0:T(128)} %param.9) | copy-start | bytes 196
  11.0 120.3 %copy-start.6 = (f32[16]{0:T(128)S(1)}, f32[16]{0:T(128)}, u32[]{:S(2)}) copy-start(f32[16]{0:T(128)} %param.8) | copy-start | bytes 196
  121.1 11.0 %copy-start = (bf16[32,512,512]{2,1,0:T(8,128)(2,1)S(1)}, bf16[32,512,512]{2,1,0:T(8,128)(2,1)}, u32[]{:S(2)}) copy-start(bf16[32,512,512]{2,1,0:T(8,128)(2,1)} %all-gather.2.cloned.1.call-done) | copy-start | bytes 50331652
  137.0 11.1 %collective-permute-start = (f32[16,8,128]{2,1,0:T(8,128)S(1)}, f32[16,8,128]{2,1,0:T(8,128)S(1)}, u32[]{:S(2)}, u32[]{:S(2)}) collective-permute-start(f32[16,8,128]{2,1,0:T(8,128)S(1)} %get-tuple-element.29), channel_id=1, source_target_pairs={{0,64},{64,0},{128,192},{192,128},{1,65},{65,1},{129,193},{193,129... | collective-permute-start | bytes 196616 | tf_op jit(solution)/shard_map/ppermute | solution.py:34
  140.6 13.6 %all-to-all-start = ((f32[4,1,16384]{2,1,0:T(1,128)}), f32[4,1,16384]{2,1,0:T(1,128)S(1)}, u32[]{:S(2)}, u32[]{:S(2)}) async-start(f32[4,1,16384]{2,1,0:T(1,128)} %reshape.42), calls=%async_computation | async-start | bytes 524288 | tf_op jit(solution)/shard_map/all_to_all | solution.py:134
  144.3 7.3 %collective-permute-start.1 = (f32[16,8,128]{2,1,0:T(8,128)S(1)}, f32[16,8,128]{2,1,0:T(8,128)S(1)}, u32[]{:S(2)}, u32[]{:S(2)}) collective-permute-start(f32[16,8,128]{2,1,0:T(8,128)S(1)} %get-tuple-element.28), channel_id=1, source_target_pairs={{0,128},{64,192},{128,0},{192,64},{1,129},{65,193},{129,1},{193,65... | collective-permute-start | bytes 196616 | tf_op jit(solution)/shard_map/ppermute | solution.py:34
  147.3 7.0 %collective-permute-start.2 = (f32[16,8,128]{2,1,0:T(8,128)S(1)}, f32[16,8,128]{2,1,0:T(8,128)S(1)}, u32[]{:S(2)}, u32[]{:S(2)}) collective-permute-start(f32[16,8,128]{2,1,0:T(8,128)S(1)} %get-tuple-element.27), channel_id=1, source_target_pairs={{0,192},{64,128},{128,64},{192,0},{1,193},{65,129},{129,65},{193,1... | collective-permute-start | bytes 196616 | tf_op jit(solution)/shard_map/ppermute | solution.py:34
  158.5 25.3 %slice-start = ((s8[16777216]{0:T(1024)(128)(4,1)}), s8[4194304]{0:T(1024)(128)(4,1)S(1)}, s32[]{:S(2)}) async-start(s8[16777216]{0:T(1024)(128)(4,1)} %bitcast.67), calls=%async_computation.5 | async-start | bytes 8388608
  173.3 10.5 %slice-start.1 = ((s8[16777216]{0:T(1024)(128)(4,1)}), s8[4194304]{0:T(1024)(128)(4,1)S(1)}, s32[]{:S(2)}) async-start(s8[16777216]{0:T(1024)(128)(4,1)} %bitcast.67), calls=%async_computation.6 | async-start | bytes 8388608
  173.4 10.4 %slice-start.2 = ((s8[16777216]{0:T(1024)(128)(4,1)}), s8[4194304]{0:T(1024)(128)(4,1)S(1)}, s32[]{:S(2)}) async-start(s8[16777216]{0:T(1024)(128)(4,1)} %bitcast.67), calls=%async_computation.7 | async-start | bytes 8388608
  178.2 5.7 %slice-start.3 = ((s8[16777216]{0:T(1024)(128)(4,1)}), s8[4194304]{0:T(1024)(128)(4,1)S(1)}, s32[]{:S(2)}) async-start(s8[16777216]{0:T(1024)(128)(4,1)} %bitcast.67), calls=%async_computation.8 | async-start | bytes 8388608
  188.7 9.9 %collective-permute-start.3 = (f32[16,8,128]{2,1,0:T(8,128)S(1)}, f32[16,8,128]{2,1,0:T(8,128)S(1)}, u32[]{:S(2)}, u32[]{:S(2)}) collective-permute-start(f32[16,8,128]{2,1,0:T(8,128)S(1)} %get-tuple-element.25), channel_id=1, source_target_pairs={{0,64},{64,0},{128,192},{192,128},{1,65},{65,1},{129,193},{193,129... | collective-permute-start | bytes 196616 | tf_op jit(solution)/shard_map/ppermute | solution.py:34
  191.4 12.4 %all-to-all-start.2 = ((f32[4,1,16384]{2,1,0:T(1,128)}), f32[4,1,16384]{2,1,0:T(1,128)S(1)}, u32[]{:S(2)}, u32[]{:S(2)}) async-start(f32[4,1,16384]{2,1,0:T(1,128)} %reshape.44), calls=%async_computation.2 | async-start | bytes 524288 | tf_op jit(solution)/shard_map/all_to_all | solution.py:134
  194.8 6.2 %collective-permute-start.4 = (f32[16,8,128]{2,1,0:T(8,128)S(1)}, f32[16,8,128]{2,1,0:T(8,128)S(1)}, u32[]{:S(2)}, u32[]{:S(2)}) collective-permute-start(f32[16,8,128]{2,1,0:T(8,128)S(1)} %get-tuple-element.24), channel_id=1, source_target_pairs={{0,128},{64,192},{128,0},{192,64},{1,129},{65,193},{129,1},{193,65... | collective-permute-start | bytes 196616 | tf_op jit(solution)/shard_map/ppermute | solution.py:34
  197.7 6.1 %collective-permute-start.5 = (f32[16,8,128]{2,1,0:T(8,128)S(1)}, f32[16,8,128]{2,1,0:T(8,128)S(1)}, u32[]{:S(2)}, u32[]{:S(2)}) collective-permute-start(f32[16,8,128]{2,1,0:T(8,128)S(1)} %get-tuple-element.23), channel_id=1, source_target_pairs={{0,192},{64,128},{128,64},{192,0},{1,193},{65,129},{129,65},{193,1... | collective-permute-start | bytes 196616 | tf_op jit(solution)/shard_map/ppermute | solution.py:34
  211.7 46.7 %all-to-all-start.3 = ((f32[64,16,128]{2,1,0:T(8,128)}), f32[64,16,128]{2,1,0:T(8,128)S(1)}, u32[]{:S(2)}, u32[]{:S(2)}) async-start(f32[64,16,128]{2,1,0:T(8,128)} %pad_maximum_fusion.1), calls=%async_computation.3 | async-start | bytes 1048576 | tf_op jit(solution)/shard_map/all_to_all | solution.py:52
Sparse Core Ops, SparseCore 0:
  11.2 109.8 all-gather.1
